TPU v7x, 256 devices: a 2x2x32 block of a 4x8x32 slice. The times are simulated.
256 devices in a mesh: groups: 4 (over y, x), pb: 64 (over z, core).
Axes of the slice: x: 2, y: 2, z: 32, core: 2. Of those that a mesh axis runs over, the one named last changes fastest.
The devices are a block of a 4x8x32 slice.
Arguments:
- eigvec: bfloat16 [65536, 2592], P(('groups', 'pb')), parts along dimension 0, may hold values from -0.69921875 to 0.69921875
- omega: bfloat16 [65536, 36], P(('groups', 'pb')), parts along dimension 0, may hold values from 0.5 to 4
- phi: bfloat16 [36, 36, 36], replicated, may hold values from -6 to 6
- send_rows: int32 [256, 128], P(('groups', 'pb')), parts along dimension 0, may hold values from 0 to 255
- local_q: int32 [4096], P(('groups', 'pb')), parts along dimension 0, may hold values from 0 to 255
- partner_q: int32 [4096], P(('groups', 'pb')), parts along dimension 0, may hold values from 0 to 255
- slot_ref: int32 [4096], P(('groups', 'pb')), parts along dimension 0, may hold values from 0 to 127, as said below
- tri_count: int32 [256], P(('groups', 'pb')), parts along dimension 0, may hold values from 8 to 16, as said below
Outputs:
- rates: float32 [36, 65536], P(None, ('groups', 'pb')), parts along dimension 1
There are 4 independent parts, one for each index of `groups`. A program takes and returns all parts, laid end to end along the dimension named above; an argument that names none is the same for every part. Nothing has to cross between parts.
Inputs may be any that keep to these rules, and one draw needn't show every extreme that they name: slot_ref of a live triplet of device p names an owner o and a slot s below the number of slots that o fills for p, which is 1 to 2; each device receives 2 filled slots from some owner. `tri_count`: exactly one device has 16 live triplets; live triplets come first.
All inputs are finite; a program needn't handle non-finite values.
Results may differ from a plain program's by a relative error of at most 0.00048.
Values may be sent and summed in bfloat16 or wider, within the bound.
A program may use at most 128 MiB of HBM per device.

v0:
```python
import jax
import jax.numpy as jnp
from jax import lax
from jax.sharding import PartitionSpec as P

NB = 36
BLK = 16


smear_width = 0.5


def sent_together(arrays, axis, split_dim, concat_dim, along):
    both = jnp.concatenate(arrays, axis=along)
    filled, at, done = (
        lax.all_to_all(both, axis, split_axis=split_dim, concat_axis=concat_dim, tiled=True),
        0,
        [],
    )
    for a in arrays:
        done.append(lax.slice_in_dim(filled, at, at + a.shape[along], axis=along))
        at += a.shape[along]
    return tuple(done)


def triplet_rates(
    phi, near_vec, partner_vec, far_vec, near_freq, partner_freq, far_freq, weight_mask
):
    y_real = jnp.einsum("abc,tnc->tabn", phi, far_vec[:, 0], preferred_element_type=jnp.float32)
    y_imag = -jnp.einsum("abc,tnc->tabn", phi, far_vec[:, 1], preferred_element_type=jnp.float32)
    y_real = y_real.astype(jnp.bfloat16)
    y_imag = y_imag.astype(jnp.bfloat16)
    part_real = partner_vec[:, 0]
    part_imag = partner_vec[:, 1]
    z_real = jnp.einsum(
        "tmb,tabn->tamn", part_real, y_real, preferred_element_type=jnp.float32
    ) - jnp.einsum("tmb,tabn->tamn", part_imag, y_imag, preferred_element_type=jnp.float32)
    z_imag = jnp.einsum(
        "tmb,tabn->tamn", part_real, y_imag, preferred_element_type=jnp.float32
    ) + jnp.einsum("tmb,tabn->tamn", part_imag, y_real, preferred_element_type=jnp.float32)
    z_real = z_real.astype(jnp.bfloat16)
    z_imag = z_imag.astype(jnp.bfloat16)
    near_real = near_vec[:, 0]
    near_imag = near_vec[:, 1]
    v_real = jnp.einsum(
        "tva,tamn->tvmn", near_real, z_real, preferred_element_type=jnp.float32
    ) - jnp.einsum("tva,tamn->tvmn", near_imag, z_imag, preferred_element_type=jnp.float32)
    v_imag = jnp.einsum(
        "tva,tamn->tvmn", near_real, z_imag, preferred_element_type=jnp.float32
    ) + jnp.einsum("tva,tamn->tvmn", near_imag, z_real, preferred_element_type=jnp.float32)
    power = v_real * v_real + v_imag * v_imag
    first = near_freq.astype(jnp.float32)[:, :, None, None]
    second = partner_freq.astype(jnp.float32)[:, None, :, None]
    third = far_freq.astype(jnp.float32)[:, None, None, :]
    offset = (first + second - third) / smear_width
    weight = jnp.exp(-offset * offset) / (first * second * third * NB)
    terms = power * weight * weight_mask[:, None, None, None]
    return (jnp.sum(terms, axis=(2, 3)), jnp.sum(terms, axis=(1, 2)))


def on_device(eigvec, omega, phi, send_rows, local_q, partner_q, slot_ref, tri_count):
    owned = eigvec.shape[0]
    outgoing = send_rows[0]
    sent_vec = jnp.take(eigvec, outgoing, axis=0)
    sent_freq = jnp.take(omega, outgoing, axis=0)
    far_vecs, far_freqs = sent_together((sent_vec, sent_freq), "pb", 0, 0, 1)
    live = tri_count[0]
    tri_slots = local_q.shape[0]
    empty = jnp.zeros((tri_slots, NB), jnp.float32)

    def one_block(block, carry):
        start = block * BLK
        weight_mask = (start + jnp.arange(BLK, dtype=jnp.int32) < live).astype(jnp.float32)
        near_vec = jnp.take(eigvec, local_q, axis=0).reshape(BLK, 2, NB, NB)
        partner_vec = jnp.take(eigvec, partner_q, axis=0).reshape(BLK, 2, NB, NB)
        far_vec = jnp.take(far_vecs, slot_ref, axis=0).reshape(BLK, 2, NB, NB)
        near_part, far_part = triplet_rates(
            phi,
            near_vec,
            partner_vec,
            far_vec,
            jnp.take(omega, local_q, axis=0),
            jnp.take(omega, partner_q, axis=0),
            jnp.take(far_freqs, slot_ref, axis=0),
            weight_mask,
        )
        return (near_part, far_part)

    upper = (live + BLK - 1) // BLK
    near_terms, far_terms = lax.fori_loop(0, upper, one_block, (empty, empty))
    by_slot = jnp.zeros((NB, outgoing.shape[0]), jnp.float32)
    by_slot = by_slot.at[:, slot_ref].add(far_terms.T)
    returned = lax.all_to_all(by_slot, "pb", split_axis=1, concat_axis=1, tiled=True)
    rates = jnp.zeros((NB, owned), jnp.float32)
    rates = rates.at[:, local_q].add(near_terms.T)
    rates = rates.at[:, outgoing].add(returned)
    return rates


def solution(mesh):
    in_specs = (
        P(("groups", "pb"), None),
        P(("groups", "pb"), None),
        P(),
        P(("groups", "pb"), None),
        P(("groups", "pb")),
        P(("groups", "pb")),
        P(("groups", "pb")),
        P(("groups", "pb")),
    )
    out_specs = P(None, ("groups", "pb"))
    return jax.shard_map(
        on_device, mesh=mesh, in_specs=in_specs, out_specs=out_specs, check_vma=False
    )
```

profile of v0, /device:TPU:37, one launch (start us, length us, event | category | flops | bytes accessed | tf_op | source)
XLA Modules:
  0.0 261.8 jit_solution(6180850608783385915)
XLA Ops:
  0.0 0.7 fusion.20
  0.7 0.5 broadcast.273
  1.2 1.3 reduce.3
  2.7 0.9 copy.30
  3.6 1.8 copy.29
  5.4 0.7 gather_fusion.1
  6.1 1.0 gather_fusion
  7.2 0.3 gather.35
  7.4 0.1 broadcast_select_fusion.3
  7.6 0.7 broadcast_select_fusion
  8.3 1.8 pad_maximum_fusion
  10.1 34.3 %all-to-all-start = ((bf16[64,2,2628]{2,1,0:T(2,128)(2,1)}), bf16[64,2,2628]{2,1,0:T(2,128)(2,1)S(1)}, u32[]{:S(2)}, u32[]{:S(2)}) async-start(bf16[64,2,2628]{2,1,0:T(2,128)(2,1)} %pad_maximum_fusion), calls=%async_computation | async-start | bytes 1376256 | tf_op jit(solution)/shard_map/all_to_all | solution.py:16
  45.1 0.6 gather_fusion.6
  45.7 0.6 gather_fusion.5
  46.3 0.6 gather_fusion.7
  46.9 0.6 gather_fusion.4
  47.6 0.5 copy-done.7
  48.3 73.7 %all-to-all-done = bf16[64,2,2628]{2,1,0:T(2,128)(2,1)S(1)} async-done(((bf16[64,2,2628]{2,1,0:T(2,128)(2,1)}), bf16[64,2,2628]{2,1,0:T(2,128)(2,1)S(1)}, u32[]{:S(2)}, u32[]{:S(2)}) %all-to-all-start) | async-done | bytes 672800 | tf_op jit(solution)/shard_map/all_to_all | solution.py:16
  122.0 0.5 all_to_all.15
  122.6 0.6 gather_fusion.3
  123.1 0.6 gather_fusion.2
  123.8 0.6 broadcast_in_dim.78.clone
  124.3 0.6 broadcast_in_dim.78
  125.0 101.9 %while.15 = (s32[]{:T(128)}, f32[16,36]{1,0:T(8,128)}, f32[16,36]{1,0:T(8,128)}, s32[]{:T(128)}, s32[16]{0:T(128)S(1)}, /*index=5*/bf16[16,2592]{1,0:T(8,128)(2,...) while((s32[]{:T(128)}, f32[16,36]{1,0:T(8,128)}, ...), condition=%wide.region_3.6_spmd, body=%wide.region_0.5_spmd.sunk | while | flops 554730752 | bytes 100491320 | solution.py:90
  125.0 0.7 compare_convert_fusion.2
  125.7 0.4 reshape.252
  126.1 0.4 reshape.251
  126.5 0.4 gather.63
  127.1 0.1 broadcast_add_fusion.2
  127.2 4.3 %fusion.58 = bf16[16,36,36,36]{2,3,1,0:T(8,128)(2,1)} fusion(bf16[36,36,36]{2,1,0:T(8,128)(2,1)S(1)} %get-tuple-element.391, bf16[16,2,36,36]{3,2,0,1:T(8,128)(2,1)S(1)} %copy_select_fusion.2), kind=kOutput, calls=%fused_computation.19.clone.1 | convolution fusion | flops 55240704 | bytes 2025472 | tf_op jit(solution)/shard_map/while/body/abc,tnc->tabn/dot_general | solution.py:30
  131.5 1.7 convolution_convert_fusion.2
  133.2 2.5 copy-done
  135.7 5.3 %fusion.61 = f32[16,36,36,36]{3,2,1,0:T(8,128)} fusion(bf16[16,36,36,36]{3,1,2,0:T(8,128)(2,1)S(1)} %convolution_convert_fusion.2, bf16[16,2,36,36]{3,2,1,0:T(8,128)(2,1)S(1)} %reshape.251), kind=kOutput, calls=%fused_computation.24.clone.1 | convolution fusion | flops 53747712 | bytes 9048064 | tf_op jit(solution)/shard_map/while/body/tmb,tabn->tamn/dot_general | solution.py:35
  141.0 10.2 %fusion.62 = bf16[16,36,36,36]{2,3,1,0:T(8,128)(2,1)} fusion(f32[16,36,36,36]{3,2,1,0:T(8,128)} %fusion.61, bf16[16,36,36,36]{2,3,1,0:T(8,128)(2,1)} %fusion.58, bf16[16,2,36,36]{3,2,1,0:T(8,128)(2,1)S(1)} %reshape.251), kind=kOutput, calls=%fused_computation.20.clone.1 | convolution fusion | flops 55240704 | bytes 6135808 | tf_op jit(solution)/shard_map/while/body/tmb,tabn->tamn/dot_general | solution.py:37
  151.2 9.8 %copy.52 = bf16[16,36,36,36]{1,3,2,0:T(8,128)(2,1)} copy(bf16[16,36,36,36]{2,3,1,0:T(8,128)(2,1)} %fusion.62) | data formatting | bytes 2985984 | tf_op jit(solution)/shard_map/while/body/convert_element_type | solution.py:41
  161.1 8.7 %fusion.57 = f32[16,36,36,36]{3,2,1,0:T(8,128)} fusion(bf16[16,36,36,36]{3,1,2,0:T(8,128)(2,1)} %copy-done, bf16[16,2,36,36]{3,2,1,0:T(8,128)(2,1)S(1)} %reshape.251), kind=kOutput, calls=%fused_computation.22.clone.1 | convolution fusion | flops 53747712 | bytes 4642816 | tf_op jit(solution)/shard_map/while/body/tmb,tabn->tamn/dot_general | solution.py:40
  169.8 10.3 %fusion.59 = bf16[16,36,36,36]{2,3,1,0:T(8,128)(2,1)} fusion(f32[16,36,36,36]{3,2,1,0:T(8,128)} %fusion.57, bf16[16,36,36,36]{2,3,1,0:T(8,128)(2,1)} %fusion.58, bf16[16,2,36,36]{3,2,1,0:T(8,128)(2,1)S(1)} %reshape.251), kind=kOutput, calls=%fused_computation.21.clone.1 | convolution fusion | flops 55240704 | bytes 6135808 | tf_op jit(solution)/shard_map/while/body/tmb,tabn->tamn/dot_general | solution.py:38
  180.1 9.9 %copy.51 = bf16[16,36,36,36]{1,3,2,0:T(8,128)(2,1)} copy(bf16[16,36,36,36]{2,3,1,0:T(8,128)(2,1)} %fusion.59) | data formatting | bytes 2985984 | tf_op jit(solution)/shard_map/while/body/convert_element_type | solution.py:42
  190.0 8.9 %fusion.64 = f32[16,36,36,36]{3,2,1,0:T(8,128)} fusion(bf16[16,36,36,36]{1,3,2,0:T(8,128)(2,1)} %copy.51, bf16[16,2,36,36]{3,2,1,0:T(8,128)(2,1)S(1)} %reshape.252), kind=kOutput, calls=%fused_computation.40.clone.1 | convolution fusion | flops 53747712 | bytes 4642816 | tf_op jit(solution)/shard_map/while/body/tva,tamn->tvmn/dot_general | solution.py:47
  198.9 5.2 %fusion.60 = f32[16,36,36,36]{3,2,1,0:T(8,128)} fusion(bf16[16,36,36,36]{1,3,2,0:T(8,128)(2,1)S(1)} %copy-done.1, bf16[16,2,36,36]{3,2,1,0:T(8,128)(2,1)S(1)} %reshape.252), kind=kOutput, calls=%fused_computation.38.clone.1 | convolution fusion | flops 53747712 | bytes 9048064 | tf_op jit(solution)/shard_map/while/body/tva,tamn->tvmn/dot_general | solution.py:48
  204.0 5.2 %fusion.63 = f32[16,36,36,36]{3,2,1,0:T(8,128)} fusion(bf16[16,36,36,36]{1,3,2,0:T(8,128)(2,1)S(1)} %bitcast.133, bf16[16,2,36,36]{3,2,1,0:T(8,128)(2,1)S(1)} %reshape.252), kind=kOutput, calls=%fused_computation.39.clone.1 | convolution fusion | flops 53747712 | bytes 9048064 | tf_op jit(solution)/shard_map/while/body/tva,tamn->tvmn/dot_general | solution.py:45
  209.2 17.6 %fusion.65 = (f32[16,36]{1,0:T(8,128)}, f32[16,36]{1,0:T(8,128)}) fusion(f32[16]{0:T(128)S(1)} %get-tuple-element.349, f32[16,36,36]{1,2,0:T(8,128)S(1)} %get-tuple-element.350, f32[16,36]{1,0:T(8,128)S(1)} %select_convert_fusion.2, f32[16,36,36]{1,2,0:T(8,128)S(1)} %get-tuple-element.352, f32[16,36,36,36]{3,2,1,0:T(8,128)} %fusion.60, ...), kind=kOutput, calls=%fused_computation.69.clone.1 | convolution fusion | flops 65690496 | bytes 11283456 | tf_op jit(solution)/shard_map/while/body/tva,tamn->tvmn/dot_general | solution.py:50
  226.9 1.4 scatter_custom_fusion.1
  228.3 6.9 %all-to-all-start.1 = ((f32[36,64,2]{0,2,1:T(2,128)}), f32[36,64,2]{0,2,1:T(2,128)S(1)}, u32[]{:S(2)}, u32[]{:S(2)}) async-start(f32[36,64,2]{0,2,1:T(2,128)} %bitcast.32), calls=%async_computation.1 | async-start | bytes 131072 | tf_op jit(solution)/shard_map/all_to_all | solution.py:93
  235.2 0.9 scatter_custom_fusion
  236.1 23.7 %all-to-all-done.1 = f32[36,64,2]{0,2,1:T(2,128)S(1)} async-done(((f32[36,64,2]{0,2,1:T(2,128)}), f32[36,64,2]{0,2,1:T(2,128)S(1)}, u32[]{:S(2)}, u32[]{:S(2)}) %all-to-all-start.1) | async-done | bytes 18464 | tf_op jit(solution)/shard_map/all_to_all | solution.py:93
  259.8 1.3 scatter_fusion
  261.1 0.7 copy.35
  (41 shorter events, 0.7 us)
Async XLA Ops:
  0.0 45.1 %copy-start.8 = (s32[16]{0:T(128)S(1)}, s32[16]{0:T(128)}, u32[]{:S(2)}) copy-start(s32[16]{0:T(128)} %param.18) | copy-start | bytes 196
  0.0 46.3 %copy-start.9 = (s32[16]{0:T(128)S(1)}, s32[16]{0:T(128)}, u32[]{:S(2)}) copy-start(s32[16]{0:T(128)} %param.19) | copy-start | bytes 196
  0.0 47.5 %copy-start.3 = (s32[16]{0:T(128)S(1)}, s32[16]{0:T(128)}, u32[]{:S(2)}) copy-start(s32[16]{0:T(128)} %param.20) | copy-start | bytes 196
  0.0 124.9 %copy-start.2 = (bf16[36,36,36]{2,1,0:T(8,128)(2,1)S(1)}, bf16[36,36,36]{2,1,0:T(8,128)(2,1)}, u32[]{:S(2)}) copy-start(bf16[36,36,36]{2,1,0:T(8,128)(2,1)} %param.16) | copy-start | bytes 279940
  0.7 4.7 %copy-start.4 = (s32[128]{0:T(128)}, s32[128]{0:T(128)S(1)}, u32[]{:S(2)}) copy-start(s32[128]{0:T(128)S(1)} %fusion.20) | copy-start | bytes 1540
  10.1 111.9 %all-to-all-start = ((bf16[64,2,2628]{2,1,0:T(2,128)(2,1)}), bf16[64,2,2628]{2,1,0:T(2,128)(2,1)S(1)}, u32[]{:S(2)}, u32[]{:S(2)}) async-start(bf16[64,2,2628]{2,1,0:T(2,128)(2,1)} %pad_maximum_fusion), calls=%async_computation | async-start | bytes 1376256 | tf_op jit(solution)/shard_map/all_to_all | solution.py:16
  45.1 79.9 %copy-start.6 = (s32[16]{0:T(128)}, s32[16]{0:T(128)S(1)}, u32[]{:S(2)}) copy-start(s32[16]{0:T(128)S(1)} %compare_select_fusion.5) | copy-start | bytes 196
  47.6 0.5 copy-start.7
  125.0 134.9 %copy-start.5 = (s32[128]{0:T(128)S(1)}, s32[128]{0:T(128)}, u32[]{:S(2)}) copy-start(s32[128]{0:T(128)} %copy-done.4) | copy-start | bytes 1540
  133.2 2.5 copy-start
  190.0 8.9 %copy-start.1 = (bf16[16,36,36,36]{1,3,2,0:T(8,128)(2,1)S(1)}, bf16[16,36,36,36]{1,3,2,0:T(8,128)(2,1)}, u32[]{:S(2)}) copy-start(bf16[16,36,36,36]{1,3,2,0:T(8,128)(2,1)} %copy.51) | copy-start | bytes 4478980 | tf_op jit(solution)/shard_map/while
  190.0 14.1 %slice-start = ((s8[5898240]{0:T(1024)(128)(4,1)}), s8[4194304]{0:T(1024)(128)(4,1)S(1)}, s32[]{:S(2)}) async-start(s8[5898240]{0:T(1024)(128)(4,1)} %bitcast.132), calls=%async_computation.2 | async-start | bytes 8388608 | tf_op jit(solution)/shard_map/while
  198.9 5.2 %slice-start.1 = ((s8[5898240]{0:T(1024)(128)(4,1)}), s8[1703936]{0:T(1024)(128)(4,1)S(1)}, s32[]{:S(2)}) async-start(s8[5898240]{0:T(1024)(128)(4,1)} %bitcast.132), calls=%async_computation.3 | async-start | bytes 3407872 | tf_op jit(solution)/shard_map/while
  228.3 31.5 %all-to-all-start.1 = ((f32[36,64,2]{0,2,1:T(2,128)}), f32[36,64,2]{0,2,1:T(2,128)S(1)}, u32[]{:S(2)}, u32[]{:S(2)}) async-start(f32[36,64,2]{0,2,1:T(2,128)} %bitcast.32), calls=%async_computation.1 | async-start | bytes 131072 | tf_op jit(solution)/shard_map/all_to_all | solution.py:93
where the time goes:
time: 263 us; the launch traced here: 262 us
  waiting for transfers between devices  97.4 us (37%)
  matrix products  77.4 us (29%)
  starting transfers between devices  41.3 us (16%)
  local copies, waits for them, and re-layouts  35.4 us (13%)
  other arithmetic  9.43 us (4%)
    all_to_all x1, waiting for transfers between devices, sent_together(): lax.all_to_all(both, axis, split_axis=split_dim, concat_axis=concat_dim,...  73.7 us
    all_to_all x1, starting transfers between devices, sent_together(): lax.all_to_all(both, axis, split_axis=split_dim, concat_axis=concat_dim,...  34.3 us
    all_to_all x1, waiting for transfers between devices, on_device(): lax.all_to_all(by_slot, 'pb', split_axis=1, concat_axis=1, tiled=True)  23.7 us
    dot_general x1, matrix products, triplet_rates(): jnp.einsum('tva,tamn->tvmn', near_imag, z_real, preferred_element_type=jn...  17.6 us
    dot_general x1, matrix products, triplet_rates(): jnp.einsum('tmb,tabn->tamn', part_real, y_imag, preferred_element_type=jn...  10.3 us
    dot_general x1, matrix products, triplet_rates(): jnp.einsum('tmb,tabn->tamn', part_imag, y_imag, preferred_element_type=jn...  10.2 us
    convert_element_type x1, local copies, waits for them, and re-layouts, triplet_rates(): z_imag = z_imag.astype(jnp.bfloat16)  9.9 us
    convert_element_type x1, local copies, waits for them, and re-layouts, triplet_rates(): z_real = z_real.astype(jnp.bfloat16)  9.85 us
  transfers between devices with their start and end apart: 2, of which 2 were waited for; matrix products, arithmetic and copies ran while one was open for 1% of the time, Pallas kernels for 0%

commit v1 on v0

v1 whole, which is shorter than its diff:
```python
import functools
import math

import jax
import jax.numpy as jnp
from jax import lax
from jax.experimental import pallas as pl
from jax.experimental.pallas import tpu as pltpu
from jax.sharding import PartitionSpec as P

LANES = 128
IM = 64
KP = 40
smear_width = 0.5
MESH = pl.DeviceIdType.MESH


def lane_iota(shape):
    return lax.broadcasted_iota(jnp.int32, shape, len(shape) - 1)


def shifted_window(tiles, start, width, to):
    first, at = divmod(start, LANES)
    moved = pltpu.roll(tiles(first), (to - at) % LANES, 1) if to != at else tiles(first)
    if at + width > LANES:
        after = pltpu.roll(tiles(first + 1), (to - at) % LANES, 1)
        moved = jnp.where(lane_iota(moved.shape) < to + LANES - at, moved, after)
    return moved


def spread_rows(tiles, nb, out_ref, im_at, both):
    half = nb * nb

    def put(k, value):
        count = value.shape[0]
        out_ref[k * count : (k + 1) * count, :] = value

    for k in range(nb):
        re = shifted_window(tiles, k * nb, nb, 0)
        im = shifted_window(tiles, half + k * nb, nb, im_at)
        lanes = lane_iota(re.shape)
        in_re = lanes < nb
        in_im = (lanes >= im_at) & (lanes < im_at + nb)
        put(k, jnp.where(in_re, re, jnp.where(in_im, im, 0.0)))
        if both:
            im0 = shifted_window(tiles, half + k * nb, nb, 0)
            re1 = shifted_window(tiles, k * nb, nb, im_at)
            put(KP + k, jnp.where(in_re, -im0, jnp.where(in_im, re1, 0.0)))
    zero = jnp.zeros(re.shape, jnp.float32)
    for k in range(nb, KP):
        put(k, zero)
        if both:
            put(KP + k, zero)


def picked(index_row, count):
    width = index_row.shape[1]
    hot = lax.broadcasted_iota(jnp.int32, (count, width), 0) == index_row
    return hot.astype(jnp.float32)


def rate_kernel(
    n,
    nb,
    slots,
    send_ref,
    near_ref,
    part_ref,
    phi_ref,
    rows_ref,
    local_ref,
    slot_ref,
    slot_s,
    live_s,
    out_ref,
    recv,
    mat,
    near_mat,
    far_mat,
    far_rows,
    inner,
    outer,
    second,
    near_acc,
    far_acc,
    by_slot,
    returned,
    send_sem,
    recv_sem,
    back_send,
    back_recv,
):
    me = lax.axis_index("pb")
    trip = near_ref.shape[0]
    width = send_ref.shape[2]
    freq_at = 2 * nb * nb
    quads = nb // 4

    def peer(i):
        off = (i + 1) // 2
        step = n // 2 + jnp.where(i % 2 == 0, off, -off)
        return step, lax.rem(me + step, n)

    def exchange(i):
        step, to = peer(i)
        return pltpu.make_async_remote_copy(
            src_ref=send_ref.at[to],
            dst_ref=recv.at[me],
            send_sem=send_sem.at[step],
            recv_sem=recv_sem.at[step],
            device_id={"pb": to},
            device_id_type=MESH,
        )

    def give_back(i):
        step, to = peer(i)
        return pltpu.make_async_remote_copy(
            src_ref=by_slot.at[to],
            dst_ref=returned.at[me],
            send_sem=back_send.at[step],
            recv_sem=back_recv.at[step],
            device_id={"pb": to},
            device_id_type=MESH,
        )

    barrier = pltpu.get_barrier_semaphore()

    def greet(i, carry):
        _, to = peer(i)
        pl.semaphore_signal(barrier, inc=1, device_id={"pb": to}, device_id_type=MESH)
        return carry

    lax.fori_loop(0, n - 1, greet, 0)
    pl.semaphore_wait(barrier, n - 1)

    def begin(i, carry):
        exchange(i).start()
        return carry

    lax.fori_loop(0, n - 1, begin, 0)

    def tiles_of(ref):
        return lambda k: ref[:, k * LANES : (k + 1) * LANES].astype(jnp.float32)

    near_tiles, part_tiles = tiles_of(near_ref), tiles_of(part_ref)
    spread_rows(part_tiles, nb, mat, IM, True)
    spread_rows(near_tiles, nb, near_mat, KP, False)

    rows = nb * trip
    pitch = inner.shape[0] // (2 * KP)
    zero_rows = jnp.zeros(((KP - nb) * pitch, LANES), jnp.float32)
    inner[nb * pitch : KP * pitch, :] = zero_rows
    inner[(KP + nb) * pitch : 2 * KP * pitch, :] = zero_rows
    part_re = mat[0:rows, :].astype(jnp.bfloat16)
    part_im = mat[KP * trip : KP * trip + rows, :].astype(jnp.bfloat16)

    def contract_b(a, carry):
        block = phi_ref[a].astype(jnp.float32)
        block = jnp.concatenate([block, jnp.zeros((nb, LANES - nb), jnp.float32)], axis=1)
        block = jnp.concatenate([block, jnp.zeros((KP - nb, LANES), jnp.float32)], axis=0)
        gap = jnp.zeros((IM - KP, LANES), jnp.float32)
        block = jnp.concatenate([block, gap, pltpu.roll(block, IM, 1), gap], axis=0)
        block = block.astype(jnp.bfloat16)
        for part, first in ((part_re, 0), (part_im, KP)):
            at = pl.multiple_of((first + a) * pitch, 8)
            inner[pl.ds(at, rows), :] = jnp.dot(
                part, block, preferred_element_type=jnp.float32
            )
        return carry

    lax.fori_loop(0, nb, contract_b, 0)

    def contract_a(t, carry):
        left = near_mat[pl.ds(t, KP, stride=trip), :]
        left = left[:, 0 : 2 * KP].astype(jnp.bfloat16)
        for quad in range(quads):
            halves = []
            for pair in range(2):
                sides = []
                for one in range(2):
                    m = quad * 4 + pair * 2 + one
                    sides.append(
                        inner[pl.ds(m * trip + t, 2 * KP, stride=pitch), :].astype(
                            jnp.bfloat16
                        )
                    )
                right = jnp.concatenate(sides, axis=1)
                halves.append(jnp.dot(left, right, preferred_element_type=jnp.float32))
            outer[t, quad * 2 * KP : (quad + 1) * 2 * KP, :] = jnp.concatenate(
                halves, axis=0
            ).astype(jnp.bfloat16)
        return carry

    lax.fori_loop(0, trip, contract_a, 0)

    low = freq_at // LANES * LANES
    at = freq_at - low
    part_freq = pltpu.roll(part_tiles(low // LANES), LANES - at, 1)
    near_freq = pltpu.roll(near_tiles(low // LANES), LANES - at, 1)
    second[...] = jnp.where(lane_iota(part_freq.shape) < nb, part_freq, 1.0)
    near_col = jnp.transpose(
        jnp.concatenate([near_freq, jnp.ones((LANES - trip, LANES), jnp.float32)], axis=0)
    )[0:KP]

    recv[me] = send_ref[me]

    def arrived(i, carry):
        copy = exchange(i)
        copy.wait_send()
        copy.wait_recv()
        return carry

    lax.fori_loop(0, n - 1, arrived, 0)

    for t in range(trip):
        where = slot_s[t]
        pair = recv[where // slots].astype(jnp.float32)
        row = pair[0:1]
        for s in range(1, slots):
            row = jnp.where(where % slots == s, pair[s : s + 1], row)
        far_rows[t : t + 1, :] = row

    far_tiles = tiles_of(far_rows)
    spread_rows(far_tiles, nb, far_mat, IM, True)
    far_freq = pltpu.roll(far_tiles(low // LANES), LANES - at, 1)
    lanes = lane_iota(far_freq.shape)
    far_freq = jnp.where(
        lanes < KP,
        far_freq,
        pltpu.roll(far_freq, KP, 1),
    )
    used = (lanes < nb) | ((lanes >= KP) & (lanes < KP + nb))
    far_freq = jnp.where(used, far_freq, 1.0)
    used_row = used[0:1]
    used_cell = (lax.broadcasted_iota(jnp.int32, (KP, LANES), 0) < nb) & (
        jnp.broadcast_to(used_row.astype(jnp.int32), (KP, LANES)) > 0
    )
    scale = math.sqrt(math.log2(math.e)) / smear_width
    live = live_s[0]

    for t in range(trip):
        ef = far_mat[pl.ds(t, 2 * KP, stride=trip), :]
        zero = jnp.zeros((2 * KP, LANES), jnp.float32)
        gap = jnp.zeros((LANES - 2 * KP, 2 * LANES), jnp.float32)
        ef = jnp.concatenate(
            [
                jnp.concatenate([ef, zero], axis=1),
                gap,
                jnp.concatenate([zero, ef], axis=1),
                gap,
            ],
            axis=0,
        ).astype(jnp.bfloat16)
        w1 = jnp.broadcast_to(near_col[:, t : t + 1], (KP, LANES))
        w3 = jnp.broadcast_to(far_freq[t : t + 1, :], (KP, LANES))
        base = (w1 - w3) * scale
        total = jnp.zeros((KP, LANES), jnp.float32)
        v = lax.dot_general(
            outer[t], ef, (((1,), (1,)), ((), ())), preferred_element_type=jnp.float32
        )
        for m in range(nb):
            w2 = jnp.broadcast_to(second[t : t + 1, m : m + 1], (KP, LANES))
            one = v[m // 2 * KP : (m // 2 + 1) * KP, (m % 2) * LANES : (m % 2 + 1) * LANES]
            x = base + w2 * scale
            total = total + one * one * (jnp.exp2(-(x * x)) / w2)
        keep = used_cell & (t < live)
        total = jnp.where(keep, total / (w1 * w3 * nb), 0.0)
        near_sum = jnp.sum(total, axis=1, keepdims=True)
        near_acc[t] = jnp.broadcast_to(near_sum, (KP, LANES))
        far_sum = jnp.sum(total, axis=0, keepdims=True)
        far_sum = far_sum + pltpu.roll(far_sum, LANES - KP, 1)
        far_acc[t : t + 1, :] = jnp.where(lane_iota(far_sum.shape) < nb, far_sum, 0.0)

    spots = lax.broadcasted_iota(jnp.int32, (n, LANES), 0)
    back = jnp.zeros((n, LANES), jnp.float32)
    for t in range(trip):
        where = slot_s[t]
        row = far_acc[t : t + 1, :]
        for s in range(1, slots):
            row = jnp.where(where % slots == s, pltpu.roll(row, s * LANES // slots, 1), row)
        back = back + jnp.where(spots == where // slots, row, 0.0)
    by_slot[...] = back.reshape(n, 1, LANES)
    returned[me] = by_slot[me]

    def begin_back(i, carry):
        give_back(i).start()
        return carry

    lax.fori_loop(0, n - 1, begin_back, 0)

    owned = out_ref.shape[1]
    columns = lane_iota((1, owned))
    rates = jnp.zeros((KP, owned), jnp.float32)
    for t in range(trip):
        spread = jnp.concatenate([near_acc[t]] * (owned // LANES), axis=1)
        rates = rates + jnp.where(columns == local_ref[0:1, t : t + 1], spread, 0.0)

    def arrived_back(i, carry):
        copy = give_back(i)
        copy.wait_send()
        copy.wait_recv()
        return carry

    lax.fori_loop(0, n - 1, arrived_back, 0)

    filled = returned[...].reshape(n, LANES)
    filled_t = jnp.transpose(jnp.concatenate([filled] * (LANES // n), axis=0))
    step = LANES // slots
    for s in range(slots):
        hot = (
            lax.broadcasted_iota(jnp.int32, (owned, LANES), 0) == rows_ref[s : s + 1, :]
        ).astype(jnp.float32)
        rates = rates + lax.dot_general(
            filled_t[s * step : s * step + KP],
            hot,
            (((1,), (1,)), ((), ())),
            precision=lax.Precision.HIGHEST,
            preferred_element_type=jnp.float32,
        )
    out_ref[...] = rates[0:nb]


def on_device(n, eigvec, omega, phi, send_rows, local_q, partner_q, slot_ref, tri_count):
    owned = eigvec.shape[0]
    nb = omega.shape[1]
    trip = local_q.shape[0]
    outgoing = send_rows[0]
    slots = outgoing.shape[0] // n
    width = -(-(eigvec.shape[1] + nb) // LANES) * LANES

    table = jnp.concatenate(
        [
            eigvec,
            omega,
            jnp.zeros((owned, width - eigvec.shape[1] - nb), eigvec.dtype),
        ],
        axis=1,
    )

    def rows_of(index):
        return jnp.take(table, index, axis=0, mode="clip")

    send = rows_of(outgoing).reshape(n, slots, width)
    near, part = rows_of(local_q), rows_of(partner_q)
    places = outgoing.reshape(n, slots).T
    places = jnp.concatenate(
        [places, jnp.full((slots, LANES - n), -1, jnp.int32)], axis=1
    )
    vmem = pl.BlockSpec(memory_space=pltpu.VMEM)
    smem = pl.BlockSpec(memory_space=pltpu.SMEM)
    f32 = jnp.float32
    return pl.pallas_call(
        functools.partial(rate_kernel, n, nb, slots),
        out_shape=jax.ShapeDtypeStruct((nb, owned), f32),
        in_specs=[vmem] * 7 + [smem] * 2,
        out_specs=vmem,
        scratch_shapes=[
            pltpu.VMEM((n, slots, width), jnp.bfloat16),
            pltpu.VMEM((2 * KP * trip, LANES), f32),
            pltpu.VMEM((KP * trip, LANES), f32),
            pltpu.VMEM((2 * KP * trip, LANES), f32),
            pltpu.VMEM((trip, width), f32),
            pltpu.VMEM((2 * KP * (nb * trip + 8), LANES), f32),
            pltpu.VMEM((trip, nb // 2 * KP, 2 * LANES), jnp.bfloat16),
            pltpu.VMEM((trip, LANES), f32),
            pltpu.VMEM((trip, KP, LANES), f32),
            pltpu.VMEM((trip, LANES), f32),
            pltpu.VMEM((n, 1, LANES), f32),
            pltpu.VMEM((n, 1, LANES), f32),
            pltpu.SemaphoreType.DMA((n,)),
            pltpu.SemaphoreType.DMA((n,)),
            pltpu.SemaphoreType.DMA((n,)),
            pltpu.SemaphoreType.DMA((n,)),
        ],
        compiler_params=pltpu.CompilerParams(
            collective_id=0, has_side_effects=True, vmem_limit_bytes=60 * 1024 * 1024
        ),
    )(
        send,
        near,
        part,
        phi,
        places,
        local_q.reshape(1, trip),
        slot_ref.reshape(1, trip),
        slot_ref,
        tri_count,
    )


def solution(mesh):
    in_specs = (
        P(("groups", "pb"), None),
        P(("groups", "pb"), None),
        P(),
        P(("groups", "pb"), None),
        P(("groups", "pb")),
        P(("groups", "pb")),
        P(("groups", "pb")),
        P(("groups", "pb")),
    )
    out_specs = P(None, ("groups", "pb"))
    return jax.shard_map(
        functools.partial(on_device, mesh.shape["pb"]),
        mesh=mesh,
        in_specs=in_specs,
        out_specs=out_specs,
        check_vma=False,
    )
```

time: 263 us -> 130 us (0.49)
  Pallas kernels: 0 us -> 118 us
  waiting for transfers between devices: 97.4 us -> 0 us
  matrix products: 77.4 us -> 0 us
  starting transfers between devices: 41.3 us -> 0 us
  local copies, waits for them, and re-layouts: 35.4 us -> 10.4 us
  other arithmetic: 9.43 us -> 0.68 us
    pallas_call x0 -> x1, Pallas kernels: none -> 118 us  [on_device(): pl.pallas_call(functools.partial(rate_kernel, n, nb, slots), out_shape=ja...]
    all_to_all x2 -> x0, waiting for transfers between devices: 97.4 us -> none  [the longest x1 73.7 us: sent_together(): lax.all_to_all(both, axis, split_axis=split_dim, concat_axis=concat_dim,...]
    dot_general x10 -> x0, matrix products: 77.4 us -> none  [the longest x1 17.6 us: triplet_rates(): jnp.einsum('tva,tamn->tvmn', near_imag, z_real, preferred_element_type=jn...]
    all_to_all x2 -> x0, starting transfers between devices: 41.3 us -> none  [the longest x1 34.3 us: sent_together(): lax.all_to_all(both, axis, split_axis=split_dim, concat_axis=concat_dim,...]
    convert_element_type x2 -> x0, local copies, waits for them, and re-layouts: 19.7 us -> none  [the longest x1 9.9 us: triplet_rates(): z_imag = z_imag.astype(jnp.bfloat16)]
    scatter-add x3 -> x0, other arithmetic: 3.56 us -> none  [the longest x1 1.4 us: on_device(): by_slot = by_slot.at[:, slot_ref].add(far_terms.T)]
    gather x10 -> x3, local copies, waits for them, and re-layouts: 5.99 us -> 3.52 us  [rows_of(): return jnp.take(table, index, axis=0, mode='clip')]
  transfers between devices with their start and end apart: 2 -> 0, of which waited for: 2 -> 0; matrix products, arithmetic and copies ran while one was open for 1% -> 0% of each run, Pallas kernels for 0% -> 0%
where the time goes in v1:
time: 130 us
  Pallas kernels  118 us (91%)
  local copies, waits for them, and re-layouts  10.4 us (8%)
    pallas_call x1, Pallas kernels, on_device(): pl.pallas_call(functools.partial(rate_kernel, n, nb, slots), out_shape=ja...  118 us
    unnamed x12, local copies, waits for them, and re-layouts  3.86 us
    gather x3, local copies, waits for them, and re-layouts, rows_of(): return jnp.take(table, index, axis=0, mode='clip')  3.52 us

profile of v1, /device:TPU:37, one launch (start us, length us, event | category | flops | bytes accessed | tf_op | source)
XLA Modules:
  0.0 129.5 jit_solution(11343176261621311132)
XLA Ops:
  0.0 0.0 copy-start
  0.0 1.8 %copy.12 = bf16[256,2592]{1,0:T(8,128)(2,1)S(1)} copy(bf16[256,2592]{0,1:T(8,128)(2,1)} %param.8) | data formatting | bytes 2654208 | tf_op args[0]
  1.8 0.0 copy-done
  1.8 0.1 copy.13
  2.0 0.0 copy-start.3
  2.0 1.1 concatenate.6
  3.1 0.0 copy-done.3
  3.1 1.0 gather_fusion
  4.2 0.0 copy-start.1
  4.2 0.0 copy-start.2
  4.2 1.1 reshape.10.send_ref
  5.3 0.0 copy-done.1
  5.3 1.2 gather_fusion.1
  6.6 0.0 copy-done.2
  6.6 1.2 gather_fusion.2
  7.8 0.5 broadcast.17
  8.3 0.7 reduce.3
  9.0 0.1 reshape_squeeze.3
  9.1 0.1 copy.14
  9.2 0.6 concatenate.7.rows_ref
  10.4 117.7 %shard_map.82 = f32[36,256]{1,0:T(8,128)} custom-call(bf16[64,2,2688]{2,1,0:T(2,128)(2,1)} %reshape.10.send_ref, bf16[16,2688]{1,0:T(8,128)(2,1)} %gather_fusion.1, bf16[16,2688]{1,0:T(8,128)(2,1)} %gather_fusion.2, bf16[36,36,36]{2,1,0:T(8,128)(2,1)} %phi_ref.1, s32[2,128]{1,0:T(2,128)} %concatenate.7.rows_ref, s32[1,16]{1,0:T(1,128)} %bitcast.6, ...), custom_call_target="tpu_custom_call" | custom-call | tf_op jit(solution)/shard_map/pallas_call | solution.py:352
  128.1 1.4 %copy.17 = f32[36,256]{1,0:T(8,128)} copy(f32[36,256]{1,0:T(8,128)} %shard_map.82) | data formatting | bytes 73728
  (4 shorter events, 0.0 us)
Async XLA Ops:
  0.0 1.8 %copy-start = (bf16[256,36]{0,1:T(8,128)(2,1)S(1)}, bf16[256,36]{0,1:T(8,128)(2,1)}, u32[]{:S(2)}) copy-start(bf16[256,36]{0,1:T(8,128)(2,1)} %param.9) | copy-start | bytes 55300
  2.0 1.1 copy-start.3
  4.2 1.1 copy-start.1
  4.2 2.4 %copy-start.2 = (s32[16]{0:T(128)S(1)}, s32[16]{0:T(128)}, u32[]{:S(2)}) copy-start(s32[16]{0:T(128)} %param.13) | copy-start | bytes 196

commit v2 on v1

--- a/solution.py
+++ b/solution.py
@@ -63,16 +63,21 @@
     n,
     nb,
     slots,
+    eig_hbm,
+    omega_ref,
+    phi_hbm,
+    rows_ref,
+    local_ref,
+    partner_ref,
+    slot_s,
+    live_s,
+    out_ref,
+    eig_ref,
+    phi_ref,
     send_ref,
     near_ref,
     part_ref,
-    phi_ref,
-    rows_ref,
-    local_ref,
-    slot_ref,
-    slot_s,
-    live_s,
-    out_ref,
+    places,
     recv,
     mat,
     near_mat,
@@ -81,6 +86,7 @@
     inner,
     outer,
     second,
+    third,
     near_acc,
     far_acc,
     by_slot,
@@ -89,48 +95,87 @@
     recv_sem,
     back_send,
     back_recv,
+    load_sem,
 ):
     me = lax.axis_index("pb")
     trip = near_ref.shape[0]
-    width = send_ref.shape[2]
+    owned = out_ref.shape[1]
     freq_at = 2 * nb * nb
     quads = nb // 4
 
     def peer(i):
         off = (i + 1) // 2
         step = n // 2 + jnp.where(i % 2 == 0, off, -off)
-        return step, lax.rem(me + step, n)
+        return lax.rem(me + step, n)
+
+    def all_moved(ref, sem):
+        every = ref.at[pl.ds(0, n - 1)]
+        pltpu.make_async_copy(every, every, sem.at[0]).wait()
 
     def exchange(i):
-        step, to = peer(i)
+        to = peer(i)
         return pltpu.make_async_remote_copy(
             src_ref=send_ref.at[to],
             dst_ref=recv.at[me],
-            send_sem=send_sem.at[step],
-            recv_sem=recv_sem.at[step],
+            send_sem=send_sem.at[0],
+            recv_sem=recv_sem.at[0],
             device_id={"pb": to},
             device_id_type=MESH,
         )
 
     def give_back(i):
-        step, to = peer(i)
+        to = peer(i)
         return pltpu.make_async_remote_copy(
             src_ref=by_slot.at[to],
             dst_ref=returned.at[me],
-            send_sem=back_send.at[step],
-            recv_sem=back_recv.at[step],
+            send_sem=back_send.at[0],
+            recv_sem=back_recv.at[0],
             device_id={"pb": to},
             device_id_type=MESH,
         )
 
+    load_eig = pltpu.make_async_copy(eig_hbm, eig_ref, load_sem.at[0])
+    load_phi = pltpu.make_async_copy(phi_hbm, phi_ref, load_sem.at[1])
+    load_eig.start()
+    load_phi.start()
     barrier = pltpu.get_barrier_semaphore()
 
     def greet(i, carry):
-        _, to = peer(i)
+        to = peer(i)
         pl.semaphore_signal(barrier, inc=1, device_id={"pb": to}, device_id_type=MESH)
         return carry
 
     lax.fori_loop(0, n - 1, greet, 0)
+
+    rest = jnp.full((1, LANES - 2 * trip), -1, jnp.int32)
+    own_row = jnp.concatenate([local_ref[...], partner_ref[...], rest], axis=1)
+    hot_send = jnp.transpose(picked(rows_ref[...], owned)).astype(jnp.bfloat16)
+    hot_own = jnp.transpose(picked(own_row, owned))[0 : 2 * trip].astype(jnp.bfloat16)
+    hot = jnp.concatenate([hot_send, hot_own], axis=0)
+    sent = n * slots
+    load_eig.wait()
+    low = freq_at // LANES * LANES
+    tail = jnp.concatenate(
+        [
+            eig_ref[low:freq_at, :].astype(jnp.float32),
+            omega_ref[...].astype(jnp.float32),
+            jnp.zeros((low + LANES - freq_at - nb, owned), jnp.float32),
+        ],
+        axis=0,
+    ).astype(jnp.bfloat16)
+    piece = 2 * LANES
+    for start in range(0, low + LANES, piece):
+        end = min(start + piece, low + LANES)
+        table = tail if start == low else eig_ref[start:end, :]
+        rows = lax.dot_general(
+            hot, table, (((1,), (1,)), ((), ())), preferred_element_type=jnp.float32
+        )
+        send_ref[:, :, start:end] = (
+            rows[0:sent].astype(jnp.bfloat16).reshape(n, slots, end - start)
+        )
+        near_ref[:, start:end] = rows[sent : sent + trip]
+        part_ref[:, start:end] = rows[sent + trip : sent + 2 * trip]
+
     pl.semaphore_wait(barrier, n - 1)
 
     def begin(i, carry):
@@ -140,7 +185,7 @@
     lax.fori_loop(0, n - 1, begin, 0)
 
     def tiles_of(ref):
-        return lambda k: ref[:, k * LANES : (k + 1) * LANES].astype(jnp.float32)
+        return lambda k: ref[:, k * LANES : (k + 1) * LANES]
 
     near_tiles, part_tiles = tiles_of(near_ref), tiles_of(part_ref)
     spread_rows(part_tiles, nb, mat, IM, True)
@@ -168,6 +213,7 @@
             )
         return carry
 
+    load_phi.wait()
     lax.fori_loop(0, nb, contract_b, 0)
 
     def contract_a(t, carry):
@@ -193,24 +239,36 @@
 
     lax.fori_loop(0, trip, contract_a, 0)
 
-    low = freq_at // LANES * LANES
+    spot = lax.broadcasted_iota(jnp.int32, (sent, sent), 0)
+    order = lane_iota((sent, sent)) == spot % n * slots + spot // n
+    places[...] = jnp.dot(
+        order.astype(jnp.bfloat16), hot_send, preferred_element_type=jnp.float32
+    ).astype(jnp.bfloat16)
+
     at = freq_at - low
+    scale = math.sqrt(math.log2(math.e)) / smear_width
     part_freq = pltpu.roll(part_tiles(low // LANES), LANES - at, 1)
     near_freq = pltpu.roll(near_tiles(low // LANES), LANES - at, 1)
-    second[...] = jnp.where(lane_iota(part_freq.shape) < nb, part_freq, 1.0)
+    part_freq = jnp.where(lane_iota(part_freq.shape) < nb, part_freq, 1.0)
+    part_scaled, part_log = part_freq * scale, -jnp.log2(part_freq)
+    first_half = lane_iota((8, LANES)) < IM
+    for t in range(trip):
+        for pair in range(nb // 2):
+            at_row = (t * (nb // 2) + pair) * 8
+            for into, of in ((second, part_scaled), (third, part_log)):
+                even = jnp.broadcast_to(of[t : t + 1, 2 * pair : 2 * pair + 1], (8, LANES))
+                odd = jnp.broadcast_to(
+                    of[t : t + 1, 2 * pair + 1 : 2 * pair + 2], (8, LANES)
+                )
+                into[at_row : at_row + 8, :] = jnp.where(first_half, even, odd)
     near_col = jnp.transpose(
         jnp.concatenate([near_freq, jnp.ones((LANES - trip, LANES), jnp.float32)], axis=0)
     )[0:KP]
 
     recv[me] = send_ref[me]
 
-    def arrived(i, carry):
-        copy = exchange(i)
-        copy.wait_send()
-        copy.wait_recv()
-        return carry
-
-    lax.fori_loop(0, n - 1, arrived, 0)
+    all_moved(recv, send_sem)
+    all_moved(recv, recv_sem)
 
     for t in range(trip):
         where = slot_s[t]
@@ -224,33 +282,24 @@
     spread_rows(far_tiles, nb, far_mat, IM, True)
     far_freq = pltpu.roll(far_tiles(low // LANES), LANES - at, 1)
     lanes = lane_iota(far_freq.shape)
-    far_freq = jnp.where(
-        lanes < KP,
-        far_freq,
-        pltpu.roll(far_freq, KP, 1),
-    )
-    used = (lanes < nb) | ((lanes >= KP) & (lanes < KP + nb))
+    far_freq = jnp.where(lanes < IM, far_freq, pltpu.roll(far_freq, IM, 1))
+    used = (lanes % IM) < nb
     far_freq = jnp.where(used, far_freq, 1.0)
-    used_row = used[0:1]
     used_cell = (lax.broadcasted_iota(jnp.int32, (KP, LANES), 0) < nb) & (
-        jnp.broadcast_to(used_row.astype(jnp.int32), (KP, LANES)) > 0
-    )
-    scale = math.sqrt(math.log2(math.e)) / smear_width
+        lane_iota((KP, LANES)) % IM < nb
+    )
     live = live_s[0]
 
     for t in range(trip):
-        ef = far_mat[pl.ds(t, 2 * KP, stride=trip), :]
-        zero = jnp.zeros((2 * KP, LANES), jnp.float32)
-        gap = jnp.zeros((LANES - 2 * KP, 2 * LANES), jnp.float32)
-        ef = jnp.concatenate(
-            [
-                jnp.concatenate([ef, zero], axis=1),
-                gap,
-                jnp.concatenate([zero, ef], axis=1),
-                gap,
-            ],
-            axis=0,
-        ).astype(jnp.bfloat16)
+        ef_re = far_mat[pl.ds(t, KP, stride=trip), :].astype(jnp.bfloat16)
+        ef_im = far_mat[pl.ds(KP * trip + t, KP, stride=trip), :].astype(jnp.bfloat16)
+        zero = jnp.zeros((IM, LANES), jnp.bfloat16)
+        cols = []
+        for ef in (ef_re, ef_im):
+            ef = jnp.concatenate([ef, zero[0 : IM - KP]], axis=0)
+            cols.append(jnp.concatenate([ef, zero], axis=1))
+            cols.append(jnp.concatenate([zero, ef], axis=1))
+        ef = jnp.concatenate(cols, axis=0)
         w1 = jnp.broadcast_to(near_col[:, t : t + 1], (KP, LANES))
         w3 = jnp.broadcast_to(far_freq[t : t + 1, :], (KP, LANES))
         base = (w1 - w3) * scale
@@ -258,17 +307,20 @@
         v = lax.dot_general(
             outer[t], ef, (((1,), (1,)), ((), ())), preferred_element_type=jnp.float32
         )
-        for m in range(nb):
-            w2 = jnp.broadcast_to(second[t : t + 1, m : m + 1], (KP, LANES))
-            one = v[m // 2 * KP : (m // 2 + 1) * KP, (m % 2) * LANES : (m % 2 + 1) * LANES]
-            x = base + w2 * scale
-            total = total + one * one * (jnp.exp2(-(x * x)) / w2)
+        for pair in range(nb // 2):
+            at_row = (t * (nb // 2) + pair) * 8
+            w2 = jnp.concatenate([second[at_row : at_row + 8, :]] * (KP // 8), axis=0)
+            log = jnp.concatenate([third[at_row : at_row + 8, :]] * (KP // 8), axis=0)
+            re = v[pair * KP : (pair + 1) * KP, 0:LANES]
+            im = v[pair * KP : (pair + 1) * KP, LANES : 2 * LANES]
+            x = base + w2
+            total = total + (re * re + im * im) * jnp.exp2(log - x * x)
         keep = used_cell & (t < live)
         total = jnp.where(keep, total / (w1 * w3 * nb), 0.0)
         near_sum = jnp.sum(total, axis=1, keepdims=True)
         near_acc[t] = jnp.broadcast_to(near_sum, (KP, LANES))
         far_sum = jnp.sum(total, axis=0, keepdims=True)
-        far_sum = far_sum + pltpu.roll(far_sum, LANES - KP, 1)
+        far_sum = far_sum + pltpu.roll(far_sum, IM, 1)
         far_acc[t : t + 1, :] = jnp.where(lane_iota(far_sum.shape) < nb, far_sum, 0.0)
 
     spots = lax.broadcasted_iota(jnp.int32, (n, LANES), 0)
@@ -288,35 +340,31 @@
 
     lax.fori_loop(0, n - 1, begin_back, 0)
 
-    owned = out_ref.shape[1]
     columns = lane_iota((1, owned))
     rates = jnp.zeros((KP, owned), jnp.float32)
     for t in range(trip):
         spread = jnp.concatenate([near_acc[t]] * (owned // LANES), axis=1)
         rates = rates + jnp.where(columns == local_ref[0:1, t : t + 1], spread, 0.0)
 
-    def arrived_back(i, carry):
-        copy = give_back(i)
-        copy.wait_send()
-        copy.wait_recv()
-        return carry
-
-    lax.fori_loop(0, n - 1, arrived_back, 0)
+    all_moved(returned, back_send)
+    all_moved(returned, back_recv)
 
     filled = returned[...].reshape(n, LANES)
-    filled_t = jnp.transpose(jnp.concatenate([filled] * (LANES // n), axis=0))
-    step = LANES // slots
-    for s in range(slots):
-        hot = (
-            lax.broadcasted_iota(jnp.int32, (owned, LANES), 0) == rows_ref[s : s + 1, :]
-        ).astype(jnp.float32)
-        rates = rates + lax.dot_general(
-            filled_t[s * step : s * step + KP],
-            hot,
-            (((1,), (1,)), ((), ())),
-            precision=lax.Precision.HIGHEST,
-            preferred_element_type=jnp.float32,
-        )
+    filled = jnp.concatenate(
+        [filled] + [pltpu.roll(filled, LANES - s * LANES // slots, 1) for s in range(1, slots)],
+        axis=0,
+    )
+    filled = jnp.transpose(filled)[0:KP]
+    parts = []
+    for _ in range(3):
+        part = filled.astype(jnp.bfloat16)
+        parts.append(part)
+        filled = filled - part.astype(jnp.float32)
+    placed = jnp.dot(
+        jnp.concatenate(parts, axis=0), places[...], preferred_element_type=jnp.float32
+    )
+    for i in range(3):
+        rates = rates + placed[i * KP : (i + 1) * KP]
     out_ref[...] = rates[0:nb]
 
 
@@ -324,37 +372,24 @@
     owned = eigvec.shape[0]
     nb = omega.shape[1]
     trip = local_q.shape[0]
-    outgoing = send_rows[0]
-    slots = outgoing.shape[0] // n
+    slots = send_rows.shape[1] // n
     width = -(-(eigvec.shape[1] + nb) // LANES) * LANES
-
-    table = jnp.concatenate(
-        [
-            eigvec,
-            omega,
-            jnp.zeros((owned, width - eigvec.shape[1] - nb), eigvec.dtype),
-        ],
-        axis=1,
-    )
-
-    def rows_of(index):
-        return jnp.take(table, index, axis=0, mode="clip")
-
-    send = rows_of(outgoing).reshape(n, slots, width)
-    near, part = rows_of(local_q), rows_of(partner_q)
-    places = outgoing.reshape(n, slots).T
-    places = jnp.concatenate(
-        [places, jnp.full((slots, LANES - n), -1, jnp.int32)], axis=1
-    )
     vmem = pl.BlockSpec(memory_space=pltpu.VMEM)
+    hbm = pl.BlockSpec(memory_space=pl.ANY)
     smem = pl.BlockSpec(memory_space=pltpu.SMEM)
     f32 = jnp.float32
     return pl.pallas_call(
         functools.partial(rate_kernel, n, nb, slots),
         out_shape=jax.ShapeDtypeStruct((nb, owned), f32),
-        in_specs=[vmem] * 7 + [smem] * 2,
+        in_specs=[hbm, vmem, hbm] + [vmem] * 3 + [smem] * 2,
         out_specs=vmem,
         scratch_shapes=[
+            pltpu.VMEM((eigvec.shape[1], owned), jnp.bfloat16),
+            pltpu.VMEM(phi.shape, jnp.bfloat16),
+            pltpu.VMEM((n, slots, width), jnp.bfloat16),
+            pltpu.VMEM((trip, width), f32),
+            pltpu.VMEM((trip, width), f32),
+            pltpu.VMEM((n * slots, owned), jnp.bfloat16),
             pltpu.VMEM((n, slots, width), jnp.bfloat16),
             pltpu.VMEM((2 * KP * trip, LANES), f32),
             pltpu.VMEM((KP * trip, LANES), f32),
@@ -362,27 +397,28 @@
             pltpu.VMEM((trip, width), f32),
             pltpu.VMEM((2 * KP * (nb * trip + 8), LANES), f32),
             pltpu.VMEM((trip, nb // 2 * KP, 2 * LANES), jnp.bfloat16),
-            pltpu.VMEM((trip, LANES), f32),
+            pltpu.VMEM((trip * nb // 2 * 8, LANES), f32),
+            pltpu.VMEM((trip * nb // 2 * 8, LANES), f32),
             pltpu.VMEM((trip, KP, LANES), f32),
             pltpu.VMEM((trip, LANES), f32),
             pltpu.VMEM((n, 1, LANES), f32),
             pltpu.VMEM((n, 1, LANES), f32),
-            pltpu.SemaphoreType.DMA((n,)),
-            pltpu.SemaphoreType.DMA((n,)),
-            pltpu.SemaphoreType.DMA((n,)),
-            pltpu.SemaphoreType.DMA((n,)),
+            pltpu.SemaphoreType.DMA((1,)),
+            pltpu.SemaphoreType.DMA((1,)),
+            pltpu.SemaphoreType.DMA((1,)),
+            pltpu.SemaphoreType.DMA((1,)),
+            pltpu.SemaphoreType.DMA((2,)),
         ],
         compiler_params=pltpu.CompilerParams(
             collective_id=0, has_side_effects=True, vmem_limit_bytes=60 * 1024 * 1024
         ),
     )(
-        send,
-        near,
-        part,
+        eigvec.T,
+        omega.T,
         phi,
-        places,
+        send_rows,
         local_q.reshape(1, trip),
-        slot_ref.reshape(1, trip),
+        partner_q.reshape(1, trip),
         slot_ref,
         tri_count,
     )

time: 130 us -> 113 us (0.87)
  local copies, waits for them, and re-layouts: 10.4 us -> 1.4 us
  Pallas kernels: 118 us -> 111 us
    pallas_call x1, Pallas kernels: 118 us -> 111 us  [on_device(): pl.pallas_call(functools.partial(rate_kernel, n, nb, slots), out_shape=ja...]
    gather x3 -> x0, local copies, waits for them, and re-layouts: 3.52 us -> none  [rows_of(): return jnp.take(table, index, axis=0, mode='clip')]
    unnamed x12 -> x1, local copies, waits for them, and re-layouts: 3.86 us -> 1.4 us
    concatenate x2 -> x0, local copies, waits for them, and re-layouts: 1.71 us -> none  [the longest x1 1.12 us: on_device(): jnp.concatenate([eigvec, omega, jnp.zeros((owned, width - eigvec.shape[1]...]
where the time goes in v2:
time: 113 us
  Pallas kernels  111 us (98%)
  local copies, waits for them, and re-layouts  1.4 us (1%)
    pallas_call x1, Pallas kernels, on_device(): pl.pallas_call(functools.partial(rate_kernel, n, nb, slots), out_shape=ja...  111 us

profile of v2, /device:TPU:37, one launch (start us, length us, event | category | flops | bytes accessed | tf_op | source)
XLA Modules:
  0.0 113.0 jit_solution(18348004691539281541)
XLA Ops:
  0.7 111.0 %shard_map.82 = f32[36,256]{1,0:T(8,128)} custom-call(bf16[2592,256]{1,0:T(8,128)(2,1)} %bitcast.4, bf16[36,256]{1,0:T(8,128)(2,1)} %bitcast.5, bf16[36,36,36]{2,1,0:T(8,128)(2,1)} %phi_hbm.1, s32[1,128]{1,0:T(1,128)} %rows_ref.1, s32[1,16]{1,0:T(1,128)} %bitcast.6, s32[1,16]{1,0:T(1,128)} %bitcast.7, s32[16]{0:T(128)} %slot_s.1, s32[1]{0:T(128)S(6)} %copy.10.live_s), custom_call_target="tpu_custom_call" | custom-call | tf_op jit(solution)/shard_map/pallas_call | solution.py:381
  111.6 1.4 %copy.11 = f32[36,256]{1,0:T(8,128)} copy(f32[36,256]{1,0:T(8,128)} %shard_map.82) | data formatting | bytes 73728

commit v3 on v2

--- a/solution.py
+++ b/solution.py
@@ -10,6 +10,7 @@
 
 LANES = 128
 IM = 64
+AHEAD = 2
 KP = 40
 smear_width = 0.5
 MESH = pl.DeviceIdType.MESH
@@ -59,26 +60,44 @@
     return hot.astype(jnp.float32)
 
 
+def waves_of(n):
+    half = n // 4
+    far, mid = half // 2 + 1, max(1, half // 4)
+    return [w for w in ((far, half), (mid, far - 1), (0, mid - 1)) if w[0] <= w[1]]
+
+
+def wave_rows(n, wave):
+    near, far = wave
+    chips = 2 * (far - near + 1) - (near == 0) - (far == n // 4)
+    return 2 * chips
+
+
 def rate_kernel(
     n,
     nb,
     slots,
     eig_hbm,
+    omega_hbm,
+    phi_hbm,
+    rows_hbm,
+    local_hbm,
+    partner_hbm,
+    slot_hbm,
+    live_hbm,
+    out_ref,
+    eig_ref,
     omega_ref,
-    phi_hbm,
+    phi_ref,
     rows_ref,
     local_ref,
     partner_ref,
     slot_s,
     live_s,
-    out_ref,
-    eig_ref,
-    phi_ref,
     send_ref,
     near_ref,
     part_ref,
     places,
-    recv,
+    recvs,
     mat,
     near_mat,
     far_mat,
@@ -89,7 +108,7 @@
     third,
     near_acc,
     far_acc,
-    by_slot,
+    by_slots,
     returned,
     send_sem,
     recv_sem,
@@ -103,49 +122,100 @@
     freq_at = 2 * nb * nb
     quads = nb // 4
 
-    def peer(i):
-        off = (i + 1) // 2
-        step = n // 2 + jnp.where(i % 2 == 0, off, -off)
-        return lax.rem(me + step, n)
-
-    def all_moved(ref, sem):
-        every = ref.at[pl.ds(0, n - 1)]
-        pltpu.make_async_copy(every, every, sem.at[0]).wait()
-
-    def exchange(i):
-        to = peer(i)
-        return pltpu.make_async_remote_copy(
-            src_ref=send_ref.at[to],
-            dst_ref=recv.at[me],
-            send_sem=send_sem.at[0],
-            recv_sem=recv_sem.at[0],
-            device_id={"pb": to},
-            device_id_type=MESH,
-        )
-
-    def give_back(i):
-        to = peer(i)
-        return pltpu.make_async_remote_copy(
-            src_ref=by_slot.at[to],
-            dst_ref=returned.at[me],
-            send_sem=back_send.at[0],
-            recv_sem=back_recv.at[0],
-            device_id={"pb": to},
-            device_id_type=MESH,
-        )
+    chips = n // 2
+    half = chips // 2
+    chip, core = me // 2, lax.rem(me, 2)
+    waves = waves_of(n)
+
+    def each(far, near, act):
+        if far == half:
+            act(half, 0)
+            act(half, 1)
+            far -= 1
+        last = max(near, 1)
+        if far >= last:
+
+            def step(i, carry):
+                d = far - i // 4
+                act(jnp.where(i % 4 < 2, d, chips - d), i % 2)
+                return carry
+
+            lax.fori_loop(0, 4 * (far - last + 1), step, 0)
+        if near == 0:
+            act(0, 1)
+
+    def device(r, c):
+        return lax.rem(chip + r, chips) * 2 + lax.rem(core + c, 2)
+
+    def seat(wave, r, c):
+        near, far = waves[wave]
+        first = far - near + 1
+        back = chips - min(far, half - 1)
+        second = chips - max(near, 1)
+        low_side = (r >= near) & (r <= far)
+        high_side = (r >= back) & (r <= second)
+        row = jnp.where(low_side, r - near, jnp.where(high_side, first + r - back, 0))
+        return row * 2 + c, low_side | high_side
+
+    def moved(ref, count, sem):
+        every = ref.at[pl.ds(0, count)]
+        pltpu.make_async_copy(every, every, sem).wait()
+
+    def exchange(wave):
+        def act(r, c):
+            to = device(r, c)
+            row, _ = seat(wave, lax.rem(chips - r, chips), c)
+            pltpu.make_async_remote_copy(
+                src_ref=send_ref.at[to],
+                dst_ref=recvs[wave].at[row],
+                send_sem=send_sem.at[0],
+                recv_sem=recv_sem.at[wave],
+                device_id={"pb": to},
+                device_id_type=MESH,
+            ).start()
+
+        return act
+
+    def give_back(wave):
+        def act(r, c):
+            to = device(r, c)
+            pltpu.make_async_remote_copy(
+                src_ref=by_slots[wave].at[to],
+                dst_ref=returned.at[me],
+                send_sem=back_send.at[0],
+                recv_sem=back_recv.at[0],
+                device_id={"pb": to},
+                device_id_type=MESH,
+            ).start()
+
+        return act
 
     load_eig = pltpu.make_async_copy(eig_hbm, eig_ref, load_sem.at[0])
     load_phi = pltpu.make_async_copy(phi_hbm, phi_ref, load_sem.at[1])
-    load_eig.start()
-    load_phi.start()
+    small = (
+        (rows_hbm, rows_ref),
+        (local_hbm, local_ref),
+        (partner_hbm, partner_ref),
+        (omega_hbm, omega_ref),
+        (slot_hbm, slot_s),
+        (live_hbm, live_s),
+    )
+    loads = [
+        pltpu.make_async_copy(source, into, load_sem.at[2 + i])
+        for i, (source, into) in enumerate(small)
+    ]
+    for load in loads + [load_eig, load_phi]:
+        load.start()
     barrier = pltpu.get_barrier_semaphore()
 
-    def greet(i, carry):
-        to = peer(i)
-        pl.semaphore_signal(barrier, inc=1, device_id={"pb": to}, device_id_type=MESH)
-        return carry
-
-    lax.fori_loop(0, n - 1, greet, 0)
+    def greet(r, c):
+        pl.semaphore_signal(
+            barrier, inc=1, device_id={"pb": device(r, c)}, device_id_type=MESH
+        )
+
+    each(half, 0, greet)
+    for load in loads:
+        load.wait()
 
     rest = jnp.full((1, LANES - 2 * trip), -1, jnp.int32)
     own_row = jnp.concatenate([local_ref[...], partner_ref[...], rest], axis=1)
@@ -178,11 +248,8 @@
 
     pl.semaphore_wait(barrier, n - 1)
 
-    def begin(i, carry):
-        exchange(i).start()
-        return carry
-
-    lax.fori_loop(0, n - 1, begin, 0)
+    for wave, (near, far) in enumerate(waves[:2]):
+        each(far, near if wave == 0 else max(near, far - AHEAD + 1), exchange(wave))
 
     def tiles_of(ref):
         return lambda k: ref[:, k * LANES : (k + 1) * LANES]
@@ -265,80 +332,93 @@
         jnp.concatenate([near_freq, jnp.ones((LANES - trip, LANES), jnp.float32)], axis=0)
     )[0:KP]
 
-    recv[me] = send_ref[me]
-
-    all_moved(recv, send_sem)
-    all_moved(recv, recv_sem)
-
-    for t in range(trip):
-        where = slot_s[t]
-        pair = recv[where // slots].astype(jnp.float32)
-        row = pair[0:1]
-        for s in range(1, slots):
-            row = jnp.where(where % slots == s, pair[s : s + 1], row)
-        far_rows[t : t + 1, :] = row
-
-    far_tiles = tiles_of(far_rows)
-    spread_rows(far_tiles, nb, far_mat, IM, True)
-    far_freq = pltpu.roll(far_tiles(low // LANES), LANES - at, 1)
-    lanes = lane_iota(far_freq.shape)
-    far_freq = jnp.where(lanes < IM, far_freq, pltpu.roll(far_freq, IM, 1))
-    used = (lanes % IM) < nb
-    far_freq = jnp.where(used, far_freq, 1.0)
-    used_cell = (lax.broadcasted_iota(jnp.int32, (KP, LANES), 0) < nb) & (
-        lane_iota((KP, LANES)) % IM < nb
-    )
-    live = live_s[0]
-
-    for t in range(trip):
-        ef_re = far_mat[pl.ds(t, KP, stride=trip), :].astype(jnp.bfloat16)
-        ef_im = far_mat[pl.ds(KP * trip + t, KP, stride=trip), :].astype(jnp.bfloat16)
-        zero = jnp.zeros((IM, LANES), jnp.bfloat16)
-        cols = []
-        for ef in (ef_re, ef_im):
-            ef = jnp.concatenate([ef, zero[0 : IM - KP]], axis=0)
-            cols.append(jnp.concatenate([ef, zero], axis=1))
-            cols.append(jnp.concatenate([zero, ef], axis=1))
-        ef = jnp.concatenate(cols, axis=0)
-        w1 = jnp.broadcast_to(near_col[:, t : t + 1], (KP, LANES))
-        w3 = jnp.broadcast_to(far_freq[t : t + 1, :], (KP, LANES))
-        base = (w1 - w3) * scale
-        total = jnp.zeros((KP, LANES), jnp.float32)
-        v = lax.dot_general(
-            outer[t], ef, (((1,), (1,)), ((), ())), preferred_element_type=jnp.float32
+    for wave, (near, far) in enumerate(waves):
+        count = recvs[wave].shape[0]
+        if near == 0:
+            recvs[wave][0] = send_ref[me]
+            count -= 1
+        moved(recvs[wave] if near else send_ref, count, recv_sem.at[wave])
+        in_wave = []
+        for t in range(trip):
+            where = slot_s[t]
+            owner = where // slots
+            seat_of, here = seat(
+                wave,
+                lax.rem(owner // 2 - chip + chips, chips),
+                lax.rem(owner + core, 2),
+            )
+            in_wave.append(here)
+            pair = recvs[wave][seat_of].astype(jnp.float32)
+            row = pair[0:1]
+            for s in range(1, slots):
+                row = jnp.where(where % slots == s, pair[s : s + 1], row)
+            far_rows[t : t + 1, :] = row
+
+        far_tiles = tiles_of(far_rows)
+        spread_rows(far_tiles, nb, far_mat, IM, True)
+        far_freq = pltpu.roll(far_tiles(low // LANES), LANES - at, 1)
+        lanes = lane_iota(far_freq.shape)
+        far_freq = jnp.where(lanes < IM, far_freq, pltpu.roll(far_freq, IM, 1))
+        used = (lanes % IM) < nb
+        far_freq = jnp.where(used, far_freq, 1.0)
+        used_cell = (lax.broadcasted_iota(jnp.int32, (KP, LANES), 0) < nb) & (
+            lane_iota((KP, LANES)) % IM < nb
         )
-        for pair in range(nb // 2):
-            at_row = (t * (nb // 2) + pair) * 8
-            w2 = jnp.concatenate([second[at_row : at_row + 8, :]] * (KP // 8), axis=0)
-            log = jnp.concatenate([third[at_row : at_row + 8, :]] * (KP // 8), axis=0)
-            re = v[pair * KP : (pair + 1) * KP, 0:LANES]
-            im = v[pair * KP : (pair + 1) * KP, LANES : 2 * LANES]
-            x = base + w2
-            total = total + (re * re + im * im) * jnp.exp2(log - x * x)
-        keep = used_cell & (t < live)
-        total = jnp.where(keep, total / (w1 * w3 * nb), 0.0)
-        near_sum = jnp.sum(total, axis=1, keepdims=True)
-        near_acc[t] = jnp.broadcast_to(near_sum, (KP, LANES))
-        far_sum = jnp.sum(total, axis=0, keepdims=True)
-        far_sum = far_sum + pltpu.roll(far_sum, IM, 1)
-        far_acc[t : t + 1, :] = jnp.where(lane_iota(far_sum.shape) < nb, far_sum, 0.0)
-
-    spots = lax.broadcasted_iota(jnp.int32, (n, LANES), 0)
-    back = jnp.zeros((n, LANES), jnp.float32)
-    for t in range(trip):
-        where = slot_s[t]
-        row = far_acc[t : t + 1, :]
-        for s in range(1, slots):
-            row = jnp.where(where % slots == s, pltpu.roll(row, s * LANES // slots, 1), row)
-        back = back + jnp.where(spots == where // slots, row, 0.0)
-    by_slot[...] = back.reshape(n, 1, LANES)
-    returned[me] = by_slot[me]
-
-    def begin_back(i, carry):
-        give_back(i).start()
-        return carry
-
-    lax.fori_loop(0, n - 1, begin_back, 0)
+        live = live_s[0]
+
+        for t in range(trip):
+            ef_re = far_mat[pl.ds(t, KP, stride=trip), :].astype(jnp.bfloat16)
+            ef_im = far_mat[pl.ds(KP * trip + t, KP, stride=trip), :].astype(jnp.bfloat16)
+            zero = jnp.zeros((IM, LANES), jnp.bfloat16)
+            cols = []
+            for ef in (ef_re, ef_im):
+                ef = jnp.concatenate([ef, zero[0 : IM - KP]], axis=0)
+                cols.append(jnp.concatenate([ef, zero], axis=1))
+                cols.append(jnp.concatenate([zero, ef], axis=1))
+            ef = jnp.concatenate(cols, axis=0)
+            w1 = jnp.broadcast_to(near_col[:, t : t + 1], (KP, LANES))
+            w3 = jnp.broadcast_to(far_freq[t : t + 1, :], (KP, LANES))
+            base = (w1 - w3) * scale
+            total = jnp.zeros((KP, LANES), jnp.float32)
+            v = lax.dot_general(
+                outer[t], ef, (((1,), (1,)), ((), ())), preferred_element_type=jnp.float32
+            )
+            for pair in range(nb // 2):
+                at_row = (t * (nb // 2) + pair) * 8
+                w2 = jnp.concatenate([second[at_row : at_row + 8, :]] * (KP // 8), axis=0)
+                log = jnp.concatenate([third[at_row : at_row + 8, :]] * (KP // 8), axis=0)
+                re = v[pair * KP : (pair + 1) * KP, 0:LANES]
+                im = v[pair * KP : (pair + 1) * KP, LANES : 2 * LANES]
+                x = base + w2
+                total = total + (re * re + im * im) * jnp.exp2(log - x * x)
+            keep = used_cell & (in_wave[t] & (t < live))
+            total = jnp.where(keep, total / (w1 * w3 * nb), 0.0)
+            near_sum = jnp.sum(total, axis=1, keepdims=True)
+            near_sum = jnp.broadcast_to(near_sum, (KP, LANES))
+            near_acc[t] = near_sum if wave == 0 else near_acc[t] + near_sum
+            far_sum = jnp.sum(total, axis=0, keepdims=True)
+            far_sum = far_sum + pltpu.roll(far_sum, IM, 1)
+            far_acc[t : t + 1, :] = jnp.where(lane_iota(far_sum.shape) < nb, far_sum, 0.0)
+
+        spots = lax.broadcasted_iota(jnp.int32, (n, LANES), 0)
+        back = jnp.zeros((n, LANES), jnp.float32)
+        for t in range(trip):
+            where = slot_s[t]
+            row = far_acc[t : t + 1, :]
+            for s in range(1, slots):
+                row = jnp.where(where % slots == s, pltpu.roll(row, s * LANES // slots, 1), row)
+            back = back + jnp.where(spots == where // slots, row, 0.0)
+        by_slots[wave][...] = back.reshape(n, 1, LANES)
+        if near == 0:
+            returned[me] = by_slots[wave][me]
+        each(far, near, give_back(wave))
+        if wave == 0:
+            for later, (start, stop) in enumerate(waves):
+                if later == 1 and stop - AHEAD >= start:
+                    each(stop - AHEAD, start, exchange(later))
+                elif later > 1:
+                    each(stop, start, exchange(later))
+    moved(send_ref, n - 1, send_sem.at[0])
 
     columns = lane_iota((1, owned))
     rates = jnp.zeros((KP, owned), jnp.float32)
@@ -346,8 +426,8 @@
         spread = jnp.concatenate([near_acc[t]] * (owned // LANES), axis=1)
         rates = rates + jnp.where(columns == local_ref[0:1, t : t + 1], spread, 0.0)
 
-    all_moved(returned, back_send)
-    all_moved(returned, back_recv)
+    moved(returned, n - 1, back_send.at[0])
+    moved(returned, n - 1, back_recv.at[0])
 
     filled = returned[...].reshape(n, LANES)
     filled = jnp.concatenate(
@@ -376,21 +456,27 @@
     width = -(-(eigvec.shape[1] + nb) // LANES) * LANES
     vmem = pl.BlockSpec(memory_space=pltpu.VMEM)
     hbm = pl.BlockSpec(memory_space=pl.ANY)
-    smem = pl.BlockSpec(memory_space=pltpu.SMEM)
     f32 = jnp.float32
+    waves = waves_of(n)
     return pl.pallas_call(
         functools.partial(rate_kernel, n, nb, slots),
         out_shape=jax.ShapeDtypeStruct((nb, owned), f32),
-        in_specs=[hbm, vmem, hbm] + [vmem] * 3 + [smem] * 2,
+        in_specs=[hbm] * 8,
         out_specs=vmem,
         scratch_shapes=[
             pltpu.VMEM((eigvec.shape[1], owned), jnp.bfloat16),
+            pltpu.VMEM((nb, owned), jnp.bfloat16),
             pltpu.VMEM(phi.shape, jnp.bfloat16),
+            pltpu.VMEM(send_rows.shape, jnp.int32),
+            pltpu.VMEM((1, trip), jnp.int32),
+            pltpu.VMEM((1, trip), jnp.int32),
+            pltpu.SMEM((trip,), jnp.int32),
+            pltpu.SMEM((1,), jnp.int32),
             pltpu.VMEM((n, slots, width), jnp.bfloat16),
             pltpu.VMEM((trip, width), f32),
             pltpu.VMEM((trip, width), f32),
             pltpu.VMEM((n * slots, owned), jnp.bfloat16),
-            pltpu.VMEM((n, slots, width), jnp.bfloat16),
+            [pltpu.VMEM((wave_rows(n, w), slots, width), jnp.bfloat16) for w in waves],
             pltpu.VMEM((2 * KP * trip, LANES), f32),
             pltpu.VMEM((KP * trip, LANES), f32),
             pltpu.VMEM((2 * KP * trip, LANES), f32),
@@ -401,13 +487,13 @@
             pltpu.VMEM((trip * nb // 2 * 8, LANES), f32),
             pltpu.VMEM((trip, KP, LANES), f32),
             pltpu.VMEM((trip, LANES), f32),
-            pltpu.VMEM((n, 1, LANES), f32),
+            [pltpu.VMEM((n, 1, LANES), f32) for _ in waves],
             pltpu.VMEM((n, 1, LANES), f32),
             pltpu.SemaphoreType.DMA((1,)),
+            pltpu.SemaphoreType.DMA((len(waves),)),
             pltpu.SemaphoreType.DMA((1,)),
             pltpu.SemaphoreType.DMA((1,)),
-            pltpu.SemaphoreType.DMA((1,)),
-            pltpu.SemaphoreType.DMA((2,)),
+            pltpu.SemaphoreType.DMA((8,)),
         ],
         compiler_params=pltpu.CompilerParams(
             collective_id=0, has_side_effects=True, vmem_limit_bytes=60 * 1024 * 1024

time: 113 us -> 115 us (1.018)
  Pallas kernels: 111 us -> 113 us
    pallas_call x1, Pallas kernels: 111 us -> 113 us  [on_device(): pl.pallas_call(functools.partial(rate_kernel, n, nb, slots), out_shape=ja...]
where the time goes in v3:
time: 115 us
  Pallas kernels  113 us (98%)
  local copies, waits for them, and re-layouts  1.4 us (1%)
    pallas_call x1, Pallas kernels, on_device(): pl.pallas_call(functools.partial(rate_kernel, n, nb, slots), out_shape=ja...  113 us

profile of v3, /device:TPU:37, one launch (start us, length us, event | category | flops | bytes accessed | tf_op | source)
XLA Modules:
  0.0 114.9 jit_solution(1179502878779928752)
XLA Ops:
  0.7 112.8 %shard_map.82 = f32[36,256]{1,0:T(8,128)} custom-call(bf16[2592,256]{1,0:T(8,128)(2,1)} %bitcast.4, bf16[36,256]{1,0:T(8,128)(2,1)} %bitcast.5, bf16[36,36,36]{2,1,0:T(8,128)(2,1)} %phi_hbm.1, s32[1,128]{1,0:T(1,128)} %rows_hbm.1, s32[1,16]{1,0:T(1,128)} %bitcast.6, s32[1,16]{1,0:T(1,128)} %bitcast.7, s32[16]{0:T(128)} %slot_hbm.1, s32[1]{0:T(128)S(6)} %copy.10.live_hbm), custom_call_target="tpu_custom_call" | custom-call | tf_op jit(solution)/shard_map/pallas_call | solution.py:461
  113.5 1.4 %copy.11 = f32[36,256]{1,0:T(8,128)} copy(f32[36,256]{1,0:T(8,128)} %shard_map.82) | data formatting | bytes 73728

commit v4 on v3

--- a/solution.py
+++ b/solution.py
@@ -10,7 +10,6 @@
 
 LANES = 128
 IM = 64
-AHEAD = 2
 KP = 40
 smear_width = 0.5
 MESH = pl.DeviceIdType.MESH
@@ -248,8 +247,8 @@
 
     pl.semaphore_wait(barrier, n - 1)
 
-    for wave, (near, far) in enumerate(waves[:2]):
-        each(far, near if wave == 0 else max(near, far - AHEAD + 1), exchange(wave))
+    for wave, (near, far) in enumerate(waves):
+        each(far, near, exchange(wave))
 
     def tiles_of(ref):
         return lambda k: ref[:, k * LANES : (k + 1) * LANES]
@@ -412,12 +411,6 @@
         if near == 0:
             returned[me] = by_slots[wave][me]
         each(far, near, give_back(wave))
-        if wave == 0:
-            for later, (start, stop) in enumerate(waves):
-                if later == 1 and stop - AHEAD >= start:
-                    each(stop - AHEAD, start, exchange(later))
-                elif later > 1:
-                    each(stop, start, exchange(later))
     moved(send_ref, n - 1, send_sem.at[0])
 
     columns = lane_iota((1, owned))

time: 115 us -> 106 us (0.922)
  Pallas kernels: 113 us -> 104 us
    pallas_call x1, Pallas kernels: 113 us -> 104 us  [on_device(): pl.pallas_call(functools.partial(rate_kernel, n, nb, slots), out_shape=ja...]
where the time goes in v4:
time: 106 us
  Pallas kernels  104 us (98%)
  local copies, waits for them, and re-layouts  1.4 us (1%)
    pallas_call x1, Pallas kernels, on_device(): pl.pallas_call(functools.partial(rate_kernel, n, nb, slots), out_shape=ja...  104 us

profile of v4, /device:TPU:37, one launch (start us, length us, event | category | flops | bytes accessed | tf_op | source)
XLA Modules:
  0.0 106.1 jit_solution(4481184703712886874)
XLA Ops:
  0.7 104.0 %shard_map.82 = f32[36,256]{1,0:T(8,128)} custom-call(bf16[2592,256]{1,0:T(8,128)(2,1)} %bitcast.4, bf16[36,256]{1,0:T(8,128)(2,1)} %bitcast.5, bf16[36,36,36]{2,1,0:T(8,128)(2,1)} %phi_hbm.1, s32[1,128]{1,0:T(1,128)} %rows_hbm.1, s32[1,16]{1,0:T(1,128)} %bitcast.6, s32[1,16]{1,0:T(1,128)} %bitcast.7, s32[16]{0:T(128)} %slot_hbm.1, s32[1]{0:T(128)S(6)} %copy.10.live_hbm), custom_call_target="tpu_custom_call" | custom-call | tf_op jit(solution)/shard_map/pallas_call | solution.py:454
  104.7 1.4 %copy.11 = f32[36,256]{1,0:T(8,128)} copy(f32[36,256]{1,0:T(8,128)} %shard_map.82) | data formatting | bytes 73728

commit v5 on v4

--- a/solution.py
+++ b/solution.py
@@ -61,8 +61,9 @@
 
 def waves_of(n):
     half = n // 4
-    far, mid = half // 2 + 1, max(1, half // 4)
-    return [w for w in ((far, half), (mid, far - 1), (0, mid - 1)) if w[0] <= w[1]]
+    cuts = [half // 2 + 1, max(1, 3 * half // 8), max(1, 3 * half // 16), 0]
+    waves = zip(cuts, [half] + [cut - 1 for cut in cuts[:-1]])
+    return [(near, far) for near, far in waves if near <= far]
 
 
 def wave_rows(n, wave):

time: 106 us -> 107 us (level)
  no operation moved by 1% of the time
where the time goes in v5:
time: 107 us
  Pallas kernels  105 us (98%)
  local copies, waits for them, and re-layouts  1.4 us (1%)
    pallas_call x1, Pallas kernels, on_device(): pl.pallas_call(functools.partial(rate_kernel, n, nb, slots), out_shape=ja...  105 us

profile of v5, /device:TPU:37, one launch (start us, length us, event | category | flops | bytes accessed | tf_op | source)
XLA Modules:
  0.0 106.8 jit_solution(13490541820692665959)
XLA Ops:
  0.7 104.7 %shard_map.82 = f32[36,256]{1,0:T(8,128)} custom-call(bf16[2592,256]{1,0:T(8,128)(2,1)} %bitcast.4, bf16[36,256]{1,0:T(8,128)(2,1)} %bitcast.5, bf16[36,36,36]{2,1,0:T(8,128)(2,1)} %phi_hbm.1, s32[1,128]{1,0:T(1,128)} %rows_hbm.1, s32[1,16]{1,0:T(1,128)} %bitcast.6, s32[1,16]{1,0:T(1,128)} %bitcast.7, s32[16]{0:T(128)} %slot_hbm.1, s32[1]{0:T(128)S(6)} %copy.10.live_hbm), custom_call_target="tpu_custom_call" | custom-call | tf_op jit(solution)/shard_map/pallas_call | solution.py:455
  105.4 1.4 %copy.11 = f32[36,256]{1,0:T(8,128)} copy(f32[36,256]{1,0:T(8,128)} %shard_map.82) | data formatting | bytes 73728
